TPU v7x, 32 devices: a whole 2x2x4 slice. The times are simulated.
32 devices in a mesh: rep: 1, dp: 32 (over x, y, z, core).
Axes of the slice: x: 2, y: 2, z: 4, core: 2. Of those that a mesh axis runs over, the one named last changes fastest.
Arguments:
- a: bfloat16 [32, 2, 4096, 1024], P(('rep', 'dp'))
- g: bfloat16 [32, 2, 4096, 3328], P(('rep', 'dp'))
Outputs:
- output: bfloat16 [2, 1024, 3328], P('rep')
All inputs are finite; a program needn't handle non-finite values.
Results may differ from a plain program's by a relative error of at most 0.012.
Values are sent between devices in bfloat16 or wider.
A program may use at most 2 GiB of HBM per device.

v0:
```python
import jax
import jax.numpy as jnp


def solution(mesh):
    groups = mesh.shape["rep"]

    def step(a, g):
        a, g = (t.reshape(groups, -1, *t.shape[1:]) for t in (a, g))
        sums = jnp.einsum("rsntd,rsntf->rndf", a, g, preferred_element_type=jnp.float32)
        return sums.astype(jnp.bfloat16).reshape(-1, *sums.shape[2:])

    return step
```

profile of v0, /device:TPU:0, one launch (start us, length us, event | category | flops | bytes accessed | tf_op | source)
XLA Modules:
  0.0 505.5 jit_solution(7434326177239353707)
XLA Ops:
  0.0 68.6 %fusion = f32[2,1024,3328]{2,1,0:T(8,128)} fusion(bf16[1,2,4096,3328]{3,2,1,0:T(8,128)(2,1)} %param.1, bf16[1,2,4096,1024]{3,2,1,0:T(8,128)(2,1)} %param), kind=kOutput, calls=%fused_computation | convolution fusion | flops 55834574848 | bytes 98566144 | tf_op jit(solution)/rsntd,rsntf->rndf/dot_general | solution.py:10
  68.6 436.9 %all-reduce.2 = bf16[2,1024,3328]{2,1,0:T(8,128)(2,1)} all-reduce(f32[2,1024,3328]{2,1,0:T(8,128)} %fusion), channel_id=1, replica_groups=mesh['axis_0'=32] {'axis_0'}, use_global_device_ids=true, to_apply=%add.clone | all-reduce | flops 6815744 | bytes 40894464 | tf_op jit(solution)/rsntd,rsntf->rndf/dot_general | solution.py:10
where the time goes:
time: 506 us; the launch traced here: 505 us
  blocking collectives  437 us (86%)
  matrix products  68.6 us (14%)
    dot_general x1, blocking collectives, step(): jnp.einsum('rsntd,rsntf->rndf', a, g, preferred_element_type=jnp.float32)  437 us
    dot_general x1, matrix products, step(): jnp.einsum('rsntd,rsntf->rndf', a, g, preferred_element_type=jnp.float32)  68.6 us

commit v1 on v0

v1 whole, which is shorter than its diff:
```python
import jax
import jax.numpy as jnp
from jax import lax
from jax.experimental import pallas as pl
from jax.experimental.pallas import tpu as pltpu
from jax.sharding import PartitionSpec as P

MESH = pl.DeviceIdType.MESH
MATS, TOKENS, D, FF = 2, 4096, 1024, 3328
COLS = 256
PER = FF // COLS
TILES = MATS * PER
HALF, QUARTER, BLOCK, PIECE = D // 2, D // 4, D // 16, D // 32
ZN = 4
GSLOTS = 3
SLOTS = 4
ZSLOTS = 8
PUTS = 8
AT = dict(a=2, z1=5, z2=8, z3=11, c=14, g0=16, g1=18, g2=21, g3=24, g4=27, g5=31, g6=33)
DN = (((0,), (0,)), ((), ()))


def kernel(
    a_hbm, g_hbm, out, av, gv, own, d_send, d_recv, a_send, a_recv, zsum, zu_send, zd_send, zu_recv, zd_recv,
    c_send, c_keep, c_recv, a_sem, g_sem, ds, dr, xs, xr, us, ur, vs, vr, cs, cr,
    gcs, gcr, gus, gur, gvs, gvr, gas, gar, gds, gdr,
):
    rep, me = lax.axis_index("rep"), lax.axis_index("dp")
    c, z = lax.rem(me, 2), lax.rem(lax.div(me, 2), ZN)
    y, x = lax.rem(lax.div(me, 8), 2), lax.div(me, 16)
    first = jnp.where(c == 0, x, y)
    third = jnp.where(c == 0, y, x)
    over_x, over_y = me + 16 * (1 - 2 * x), me + 8 * (1 - 2 * y)
    first_peer = jnp.where(c == 0, over_x, over_y)
    third_peer = jnp.where(c == 0, over_y, over_x)
    partner, above, below = me + 1 - 2 * c, me + 2, me - 2
    has_above, has_below = z < ZN - 1, z > 0

    def remote(src, dst, send, recv, dev):
        return pltpu.make_async_remote_copy(
            src_ref=src, dst_ref=dst, send_sem=send, recv_sem=recv, device_id=(rep, dev), device_id_type=MESH
        )

    def load_g(t):
        n, j = lax.div(t, PER), lax.rem(t, PER)
        s = lax.rem(t, GSLOTS)
        return pltpu.make_async_copy(
            g_hbm.at[0, n, :, pl.ds(pl.multiple_of(j * COLS, COLS), COLS)], gv.at[s], g_sem.at[s]
        )

    def load_a(k):
        cols = pl.ds(pl.multiple_of(jnp.where(k == 0, 1 - c, c) * HALF, HALF), HALF)
        return pltpu.make_async_copy(a_hbm.at[0, 0, :, cols], av.at[0, :, cols], a_sem.at[k])

    load_rest = pltpu.make_async_copy(a_hbm.at[0, 1], av.at[1], a_sem.at[2])
    load_g(0).start()
    load_a(0).start()
    load_a(1).start()
    load_g(1).start()

    barrier = pltpu.get_barrier_semaphore()
    for dev in (partner, over_x, over_y):
        pl.semaphore_signal(barrier, inc=1, device_id=(rep, dev), device_id_type=MESH)

    @pl.when(has_above)
    def _():
        pl.semaphore_signal(barrier, inc=1, device_id=(rep, above), device_id_type=MESH)

    @pl.when(has_below)
    def _():
        pl.semaphore_signal(barrier, inc=1, device_id=(rep, below), device_id_type=MESH)

    pl.semaphore_wait(barrier, 3 + has_above.astype(jnp.int32) + has_below.astype(jnp.int32))

    def rows(start, size):
        return pl.ds(pl.multiple_of(start, size), size)

    def copy_d(i):
        s = lax.rem(i, SLOTS)
        return remote(d_send.at[s], d_recv.at[i], ds.at[i], dr.at[i], partner)

    def copy_a(i):
        s = lax.rem(i, SLOTS)
        return remote(a_send.at[s], a_recv.at[i], xs.at[i], xr.at[i], first_peer)

    def copy_u(h, i):
        s = lax.rem(i, SLOTS)
        return remote(zu_send.at[h - 1, s], zu_recv.at[h - 1, i], us.at[h - 1, i], ur.at[h - 1, i], above)

    def copy_v(h, i):
        s = lax.rem(i, SLOTS)
        return remote(zd_send.at[h - 1, s], zd_recv.at[h - 1, i], vs.at[h - 1, i], vr.at[h - 1, i], below)

    def copy_c(i):
        s = lax.rem(i, SLOTS)
        return remote(c_send.at[s], c_recv.at[i], cs.at[i], cr.at[i], third_peer)

    def place(i, start, size):
        n, j = lax.div(i, PER), lax.rem(i, PER)
        return out.at[n, rows(start, size), pl.ds(pl.multiple_of(j * COLS, COLS), COLS)]

    def shared(i, start, size, send, recv, dev):
        ref = place(i, start, size)
        return remote(ref, ref, send, recv, dev)

    base_a = c * HALF + first * QUARTER
    base_c = base_a + z * BLOCK

    def copy_gc(i, mine=True):
        return shared(i, base_c + (third if mine else 1 - third) * PIECE, PIECE, gcs.at[i], gcr.at[i], third_peer)

    def copy_gu(k, i, block):
        return shared(i, base_a + block * BLOCK, BLOCK, gus.at[k - 1, i], gur.at[k - 1, i], above)

    def copy_gv(k, i, block):
        return shared(i, base_a + block * BLOCK, BLOCK, gvs.at[k - 1, i], gvr.at[k - 1, i], below)

    def copy_ga(i, mine=True):
        return shared(
            i, c * HALF + (first if mine else 1 - first) * QUARTER, QUARTER, gas.at[i], gar.at[i], first_peer
        )

    def copy_gd(i, mine=True):
        return shared(i, (c if mine else 1 - c) * HALF, HALF, gds.at[i], gdr.at[i], partner)

    def reuse(copy, i):
        @pl.when(i >= SLOTS)
        def _():
            copy(i - SLOTS).wait_send()

    def step_a(i):
        s, zs = lax.rem(i, SLOTS), lax.rem(i, ZSLOTS)
        copy_d(i).wait_recv()
        reuse(copy_a, i)
        away, keep = rows((1 - first) * QUARTER, QUARTER), rows(first * QUARTER, QUARTER)
        a_send[s] = (own[away, :] + d_recv[i, away, :].astype(jnp.float32)).astype(jnp.bfloat16)
        copy_a(i).start()
        zsum[zs] = own[keep, :] + d_recv[i, keep, :].astype(jnp.float32)

    def hop(h, i):
        s, zs = lax.rem(i, SLOTS), lax.rem(i, ZSLOTS)
        if h == 1:
            copy_a(i).wait_recv()
            zsum[zs] += a_recv[i].astype(jnp.float32)
        else:
            take(h - 1, i)
        if h == ZN:
            return

        @pl.when(jnp.logical_and(has_above, z <= h - 1))
        def _():
            reuse(lambda k: copy_u(h, k), i)
            zu_send[h - 1, s] = zsum[zs, rows((z + ZN - h) * BLOCK, BLOCK), :].astype(jnp.bfloat16)
            copy_u(h, i).start()

        @pl.when(jnp.logical_and(has_below, z >= ZN - h))
        def _():
            reuse(lambda k: copy_v(h, k), i)
            zd_send[h - 1, s] = zsum[zs, rows((z - ZN + h) * BLOCK, BLOCK), :].astype(jnp.bfloat16)
            copy_v(h, i).start()

    def take(h, i):
        zs = lax.rem(i, ZSLOTS)

        @pl.when(jnp.logical_and(has_below, z <= h))
        def _():
            copy_u(h, i).wait_recv()
            zsum[zs, rows((z + ZN - 1 - h) * BLOCK, BLOCK), :] += zu_recv[h - 1, i].astype(jnp.float32)

        @pl.when(jnp.logical_and(has_above, z >= ZN - 1 - h))
        def _():
            copy_v(h, i).wait_recv()
            zsum[zs, rows((z - ZN + 1 + h) * BLOCK, BLOCK), :] += zd_recv[h - 1, i].astype(jnp.float32)

    def step_c(i):
        s, zs = lax.rem(i, SLOTS), lax.rem(i, ZSLOTS)
        take(ZN - 1, i)
        reuse(copy_c, i)
        c_send[s] = zsum[zs, rows(z * BLOCK + (1 - third) * PIECE, PIECE), :].astype(jnp.bfloat16)
        copy_c(i).start()
        c_keep[s] = zsum[zs, rows(z * BLOCK + third * PIECE, PIECE), :]

    def step_g0(i):
        s = lax.rem(i, SLOTS)
        copy_c(i).wait_recv()
        total = c_keep[s] + c_recv[i].astype(jnp.float32)
        n, j = lax.div(i, PER), lax.rem(i, PER)
        out[n, rows(base_c + third * PIECE, PIECE), pl.ds(pl.multiple_of(j * COLS, COLS), COLS)] = total.astype(
            jnp.bfloat16
        )
        copy_gc(i).start()

    def spread(k, i):
        if k == 1:
            copy_gc(i, False).wait_recv()
        else:
            arrive(k - 1, i)

        @pl.when(jnp.logical_and(has_above, z >= k - 1))
        def _():
            copy_gu(k, i, z - k + 1).start()

        @pl.when(jnp.logical_and(has_below, z <= ZN - k))
        def _():
            copy_gv(k, i, z + k - 1).start()

    def arrive(k, i):
        @pl.when(z >= k)
        def _():
            copy_gu(k, i, z - k).wait_recv()

        @pl.when(z <= ZN - 1 - k)
        def _():
            copy_gv(k, i, z + k).wait_recv()

    def step_g4(i):
        arrive(ZN - 1, i)
        copy_ga(i).start()

    def step_g5(i):
        copy_ga(i, False).wait_recv()
        copy_gd(i).start()

    def step_g6(i):
        copy_gd(i, False).wait_recv()

    steps = dict(
        a=step_a,
        z1=lambda i: hop(1, i),
        z2=lambda i: hop(2, i),
        z3=lambda i: hop(3, i),
        c=step_c,
        g0=step_g0,
        g1=lambda i: spread(1, i),
        g2=lambda i: spread(2, i),
        g3=lambda i: spread(3, i),
        g4=step_g4,
        g5=step_g5,
        g6=step_g6,
    )
    order = sorted(steps, key=lambda name: -AT[name])

    def run(t, parity):
        for name in order:
            if AT[name] % 2 == parity:
                i = t - AT[name] // 2

                @pl.when(jnp.logical_and(i >= 0, i < TILES))
                def _():
                    steps[name](i)

    def loop(t, carry):
        run(t, 0)
        live = t < TILES
        n = lax.div(t, PER)
        gs = lax.rem(t, GSLOTS)

        @pl.when(live)
        def _():
            @pl.when(t + 2 < TILES)
            def _():
                load_g(t + 2).start()

            @pl.when(t == 2)
            def _():
                load_rest.start()

            @pl.when(t == PER)
            def _():
                load_rest.wait()

            load_g(t).wait()

            @pl.when(t == 0)
            def _():
                load_a(0).wait()

            reuse(copy_d, t)
            d_send[lax.rem(t, SLOTS)] = lax.dot_general(
                av[n, :, pl.ds(pl.multiple_of((1 - c) * HALF, HALF), HALF)],
                gv[gs],
                DN,
                preferred_element_type=jnp.float32,
            ).astype(jnp.bfloat16)
            copy_d(t).start()

        run(t, 1)

        @pl.when(live)
        def _():
            @pl.when(t == 0)
            def _():
                load_a(1).wait()

            own[...] = lax.dot_general(
                av[n, :, pl.ds(pl.multiple_of(c * HALF, HALF), HALF)],
                gv[gs],
                DN,
                preferred_element_type=jnp.float32,
            )

        return carry

    lax.fori_loop(0, TILES + max(AT.values()) // 2, loop, 0)

    def finish_staged(i, carry):
        copy_d(i).wait_send()
        copy_a(i).wait_send()
        copy_c(i).wait_send()
        for h in range(1, ZN):

            @pl.when(jnp.logical_and(has_above, z <= h - 1))
            def _():
                copy_u(h, i).wait_send()

            @pl.when(jnp.logical_and(has_below, z >= ZN - h))
            def _():
                copy_v(h, i).wait_send()

        return carry

    def finish_shared(i, carry):
        copy_gc(i).wait_send()
        copy_ga(i).wait_send()
        copy_gd(i).wait_send()
        for k in range(1, ZN):

            @pl.when(jnp.logical_and(has_above, z >= k - 1))
            def _():
                copy_gu(k, i, z - k + 1).wait_send()

            @pl.when(jnp.logical_and(has_below, z <= ZN - k))
            def _():
                copy_gv(k, i, z + k - 1).wait_send()

        return carry

    lax.fori_loop(TILES - SLOTS, TILES, finish_staged, 0)
    lax.fori_loop(0, TILES, finish_shared, 0)


def put(sums, out, sem):
    copies = []
    for k in range(MATS * PUTS):
        part = (k // PUTS, pl.ds(k % PUTS * (D // PUTS), D // PUTS))
        copies.append(pltpu.make_async_copy(sums.at[part], out.at[part], sem.at[k]))
        copies[-1].start()
    for copy in copies:
        copy.wait()


def solution(mesh):
    bf16, f32 = jnp.bfloat16, jnp.float32

    def step(a, g):
        dma = pltpu.SemaphoreType.DMA
        one, three = dma((TILES,)), dma((ZN - 1, TILES))
        scratch = [
            pltpu.VMEM((MATS, TOKENS, D), bf16),
            pltpu.VMEM((GSLOTS, TOKENS, COLS), bf16),
            pltpu.VMEM((HALF, COLS), f32),
            pltpu.VMEM((SLOTS, HALF, COLS), bf16),
            pltpu.VMEM((TILES, HALF, COLS), bf16),
            pltpu.VMEM((SLOTS, QUARTER, COLS), bf16),
            pltpu.VMEM((TILES, QUARTER, COLS), bf16),
            pltpu.VMEM((ZSLOTS, QUARTER, COLS), f32),
            pltpu.VMEM((ZN - 1, SLOTS, BLOCK, COLS), bf16),
            pltpu.VMEM((ZN - 1, SLOTS, BLOCK, COLS), bf16),
            pltpu.VMEM((ZN - 1, TILES, BLOCK, COLS), bf16),
            pltpu.VMEM((ZN - 1, TILES, BLOCK, COLS), bf16),
            pltpu.VMEM((SLOTS, PIECE, COLS), bf16),
            pltpu.VMEM((SLOTS, PIECE, COLS), f32),
            pltpu.VMEM((TILES, PIECE, COLS), bf16),
            dma((3,)),
            dma((GSLOTS,)),
        ]
        scratch += [one] * 4 + [three] * 4 + [one] * 2
        scratch += [one] * 2 + [three] * 4 + [one] * 4
        sums = pl.pallas_call(
            kernel,
            out_shape=pltpu.VMEM((MATS, D, FF), bf16),
            in_specs=[pl.BlockSpec(memory_space=pl.ANY)] * 2,
            out_specs=pl.BlockSpec(memory_space=pltpu.VMEM),
            scratch_shapes=scratch,
            compiler_params=pltpu.CompilerParams(
                collective_id=0, has_side_effects=True, vmem_limit_bytes=48 * 2**20
            ),
        )(a, g)
        return pl.pallas_call(
            put,
            out_shape=jax.ShapeDtypeStruct((MATS, D, FF), bf16),
            in_specs=[pl.BlockSpec(memory_space=pltpu.VMEM)],
            out_specs=pl.BlockSpec(memory_space=pl.ANY),
            scratch_shapes=[dma((MATS * PUTS,))],
            compiler_params=pltpu.CompilerParams(vmem_limit_bytes=2**20),
        )(sums)

    return jax.shard_map(
        step,
        mesh=mesh,
        in_specs=(P(("rep", "dp")), P(("rep", "dp"))),
        out_specs=P("rep"),
        check_vma=False,
    )
```

time: 506 us -> 141 us (0.28)
  blocking collectives: 437 us -> 0 us
  Pallas kernels: 0 us -> 141 us
  matrix products: 68.6 us -> 0 us
    dot_general x1 -> x0, blocking collectives: 437 us -> none  [step(): jnp.einsum('rsntd,rsntf->rndf', a, g, preferred_element_type=jnp.float32)]
    pallas_call x0 -> x2, Pallas kernels: none -> 141 us  [the longest x1 136 us: step(): pl.pallas_call(kernel, out_shape=pltpu.VMEM((MATS, D, FF), bf16), in_spec...]
    dot_general x1 -> x0, matrix products: 68.6 us -> none  [step(): jnp.einsum('rsntd,rsntf->rndf', a, g, preferred_element_type=jnp.float32)]
where the time goes in v1:
time: 141 us
  Pallas kernels  141 us (100%)
    pallas_call x1, Pallas kernels, step(): pl.pallas_call(kernel, out_shape=pltpu.VMEM((MATS, D, FF), bf16), in_spec...  136 us
    pallas_call x1, Pallas kernels, step(): pl.pallas_call(put, out_shape=jax.ShapeDtypeStruct((MATS, D, FF), bf16),...  5 us

profile of v1, /device:TPU:0, one launch (start us, length us, event | category | flops | bytes accessed | tf_op | source)
XLA Modules:
  0.0 140.8 jit_solution(17489019445446695527)
XLA Ops:
  0.0 135.8 %shard_map.28.sums = bf16[2,1024,3328]{2,1,0:T(8,128)(2,1)S(1)} custom-call(bf16[1,2,4096,1024]{3,2,1,0:T(8,128)(2,1)} %a_hbm.1, bf16[1,2,4096,3328]{3,2,1,0:T(8,128)(2,1)} %g_hbm.1), custom_call_target="tpu_custom_call" | custom-call | tf_op jit(solution)/shard_map/pallas_call | solution.py:379
  135.8 5.0 %shard_map.29 = bf16[2,1024,3328]{2,1,0:T(8,128)(2,1)} custom-call(bf16[2,1024,3328]{2,1,0:T(8,128)(2,1)S(1)} %shard_map.28.sums), custom_call_target="tpu_custom_call" | custom-call | tf_op jit(solution)/shard_map/pallas_call | solution.py:389

commit v2 on v1

--- a/solution.py
+++ b/solution.py
@@ -9,14 +9,18 @@
 MATS, TOKENS, D, FF = 2, 4096, 1024, 3328
 COLS = 256
 PER = FF // COLS
-TILES = MATS * PER
-HALF, QUARTER, BLOCK, PIECE = D // 2, D // 4, D // 16, D // 32
+PARTS = 1
+TILES = MATS * PER * PARTS
+CORE = D // 2
+HALF = CORE // PARTS
+QUARTER, BLOCK, PIECE = HALF // 2, HALF // 8, HALF // 16
 ZN = 4
 GSLOTS = 3
-SLOTS = 4
-ZSLOTS = 8
+SLOTS = 8
+LATE = 32
+ZSLOTS = 12
 PUTS = 8
-AT = dict(a=2, z1=5, z2=8, z3=11, c=14, g0=16, g1=18, g2=21, g3=24, g4=27, g5=31, g6=33)
+AT = dict(a=2, z1=4, z2=5, z3=7, c=9, g0=11, g1=13, g2=15, g3=17, g4=19, g5=29)
 DN = (((0,), (0,)), ((), ()))
 
 
@@ -41,21 +45,22 @@
             src_ref=src, dst_ref=dst, send_sem=send, recv_sem=recv, device_id=(rep, dev), device_id_type=MESH
         )
 
-    def load_g(t):
-        n, j = lax.div(t, PER), lax.rem(t, PER)
-        s = lax.rem(t, GSLOTS)
+    def load_g(u):
+        n, j = lax.div(u, PER), lax.rem(u, PER)
+        s = lax.rem(u, GSLOTS)
         return pltpu.make_async_copy(
             g_hbm.at[0, n, :, pl.ds(pl.multiple_of(j * COLS, COLS), COLS)], gv.at[s], g_sem.at[s]
         )
 
-    def load_a(k):
-        cols = pl.ds(pl.multiple_of(jnp.where(k == 0, 1 - c, c) * HALF, HALF), HALF)
-        return pltpu.make_async_copy(a_hbm.at[0, 0, :, cols], av.at[0, :, cols], a_sem.at[k])
-
-    load_rest = pltpu.make_async_copy(a_hbm.at[0, 1], av.at[1], a_sem.at[2])
+    def load_a(n, k):
+        cols = pl.ds(pl.multiple_of((1 - c if k == 0 else c) * CORE, CORE), CORE)
+        return pltpu.make_async_copy(
+            a_hbm.at[0, n, :, cols], av.at[n, :, k * CORE : (k + 1) * CORE], a_sem.at[n, k]
+        )
+
     load_g(0).start()
-    load_a(0).start()
-    load_a(1).start()
+    load_a(0, 0).start()
+    load_a(0, 1).start()
     load_g(1).start()
 
     barrier = pltpu.get_barrier_semaphore()
@@ -77,51 +82,55 @@
 
     def copy_d(i):
         s = lax.rem(i, SLOTS)
-        return remote(d_send.at[s], d_recv.at[i], ds.at[i], dr.at[i], partner)
+        return remote(d_send.at[s], d_recv.at[i], ds.at[s], dr.at[s], partner)
 
     def copy_a(i):
         s = lax.rem(i, SLOTS)
-        return remote(a_send.at[s], a_recv.at[i], xs.at[i], xr.at[i], first_peer)
+        return remote(a_send.at[s], a_recv.at[i], xs.at[s], xr.at[s], first_peer)
 
     def copy_u(h, i):
         s = lax.rem(i, SLOTS)
-        return remote(zu_send.at[h - 1, s], zu_recv.at[h - 1, i], us.at[h - 1, i], ur.at[h - 1, i], above)
+        return remote(zu_send.at[h - 1, s], zu_recv.at[h - 1, i], us.at[h - 1, s], ur.at[h - 1, s], above)
 
     def copy_v(h, i):
         s = lax.rem(i, SLOTS)
-        return remote(zd_send.at[h - 1, s], zd_recv.at[h - 1, i], vs.at[h - 1, i], vr.at[h - 1, i], below)
+        return remote(zd_send.at[h - 1, s], zd_recv.at[h - 1, i], vs.at[h - 1, s], vr.at[h - 1, s], below)
 
     def copy_c(i):
         s = lax.rem(i, SLOTS)
-        return remote(c_send.at[s], c_recv.at[i], cs.at[i], cr.at[i], third_peer)
+        return remote(c_send.at[s], c_recv.at[i], cs.at[s], cr.at[s], third_peer)
+
+    def spot(i):
+        n, j = lax.div(i, PER * PARTS), lax.rem(lax.div(i, PARTS), PER)
+        return n, lax.rem(i, PARTS) * HALF, pl.ds(pl.multiple_of(j * COLS, COLS), COLS)
 
     def place(i, start, size):
-        n, j = lax.div(i, PER), lax.rem(i, PER)
-        return out.at[n, rows(start, size), pl.ds(pl.multiple_of(j * COLS, COLS), COLS)]
+        n, row, cols = spot(i)
+        return out.at[n, rows(row + start, size), cols]
 
     def shared(i, start, size, send, recv, dev):
         ref = place(i, start, size)
         return remote(ref, ref, send, recv, dev)
 
-    base_a = c * HALF + first * QUARTER
+    base_a = c * CORE + first * QUARTER
     base_c = base_a + z * BLOCK
 
     def copy_gc(i, mine=True):
-        return shared(i, base_c + (third if mine else 1 - third) * PIECE, PIECE, gcs.at[i], gcr.at[i], third_peer)
+        return shared(i, base_c + (third if mine else 1 - third) * PIECE, PIECE, gcs, gcr.at[lax.rem(i, SLOTS)], third_peer)
 
     def copy_gu(k, i, block):
-        return shared(i, base_a + block * BLOCK, BLOCK, gus.at[k - 1, i], gur.at[k - 1, i], above)
+        return shared(i, base_a + block * BLOCK, BLOCK, gus.at[k - 1], gur.at[k - 1, lax.rem(i, SLOTS)], above)
 
     def copy_gv(k, i, block):
-        return shared(i, base_a + block * BLOCK, BLOCK, gvs.at[k - 1, i], gvr.at[k - 1, i], below)
+        return shared(i, base_a + block * BLOCK, BLOCK, gvs.at[k - 1], gvr.at[k - 1, lax.rem(i, SLOTS)], below)
 
     def copy_ga(i, mine=True):
         return shared(
-            i, c * HALF + (first if mine else 1 - first) * QUARTER, QUARTER, gas.at[i], gar.at[i], first_peer
+            i, c * CORE + (first if mine else 1 - first) * QUARTER, QUARTER, gas, gar.at[lax.rem(i, LATE)], first_peer
         )
 
     def copy_gd(i, mine=True):
-        return shared(i, (c if mine else 1 - c) * HALF, HALF, gds.at[i], gdr.at[i], partner)
+        return shared(i, (c if mine else 1 - c) * CORE, HALF, gds, gdr, partner)
 
     def reuse(copy, i):
         @pl.when(i >= SLOTS)
@@ -130,12 +139,13 @@
 
     def step_a(i):
         s, zs = lax.rem(i, SLOTS), lax.rem(i, ZSLOTS)
+        o = lax.rem(i, 2)
         copy_d(i).wait_recv()
         reuse(copy_a, i)
         away, keep = rows((1 - first) * QUARTER, QUARTER), rows(first * QUARTER, QUARTER)
-        a_send[s] = (own[away, :] + d_recv[i, away, :].astype(jnp.float32)).astype(jnp.bfloat16)
+        a_send[s] = (own[o, away, :] + d_recv[i, away, :].astype(jnp.float32)).astype(jnp.bfloat16)
         copy_a(i).start()
-        zsum[zs] = own[keep, :] + d_recv[i, keep, :].astype(jnp.float32)
+        zsum[zs] = own[o, keep, :] + d_recv[i, keep, :].astype(jnp.float32)
 
     def hop(h, i):
         s, zs = lax.rem(i, SLOTS), lax.rem(i, ZSLOTS)
@@ -184,10 +194,8 @@
         s = lax.rem(i, SLOTS)
         copy_c(i).wait_recv()
         total = c_keep[s] + c_recv[i].astype(jnp.float32)
-        n, j = lax.div(i, PER), lax.rem(i, PER)
-        out[n, rows(base_c + third * PIECE, PIECE), pl.ds(pl.multiple_of(j * COLS, COLS), COLS)] = total.astype(
-            jnp.bfloat16
-        )
+        n, row, cols = spot(i)
+        out[n, rows(row + base_c + third * PIECE, PIECE), cols] = total.astype(jnp.bfloat16)
         copy_gc(i).start()
 
     def spread(k, i):
@@ -220,9 +228,6 @@
     def step_g5(i):
         copy_ga(i, False).wait_recv()
         copy_gd(i).start()
-
-    def step_g6(i):
-        copy_gd(i, False).wait_recv()
 
     steps = dict(
         a=step_a,
@@ -236,72 +241,55 @@
         g3=lambda i: spread(3, i),
         g4=step_g4,
         g5=step_g5,
-        g6=step_g6,
     )
     order = sorted(steps, key=lambda name: -AT[name])
 
-    def run(t, parity):
+    def run(t):
         for name in order:
-            if AT[name] % 2 == parity:
-                i = t - AT[name] // 2
-
-                @pl.when(jnp.logical_and(i >= 0, i < TILES))
-                def _():
-                    steps[name](i)
-
-    def loop(t, carry):
-        run(t, 0)
-        live = t < TILES
-        n = lax.div(t, PER)
-        gs = lax.rem(t, GSLOTS)
-
-        @pl.when(live)
-        def _():
-            @pl.when(t + 2 < TILES)
-            def _():
-                load_g(t + 2).start()
-
-            @pl.when(t == 2)
-            def _():
-                load_rest.start()
-
-            @pl.when(t == PER)
-            def _():
-                load_rest.wait()
-
-            load_g(t).wait()
-
-            @pl.when(t == 0)
-            def _():
-                load_a(0).wait()
-
-            reuse(copy_d, t)
-            d_send[lax.rem(t, SLOTS)] = lax.dot_general(
-                av[n, :, pl.ds(pl.multiple_of((1 - c) * HALF, HALF), HALF)],
-                gv[gs],
-                DN,
-                preferred_element_type=jnp.float32,
-            ).astype(jnp.bfloat16)
-            copy_d(t).start()
-
-        run(t, 1)
-
-        @pl.when(live)
-        def _():
-            @pl.when(t == 0)
-            def _():
-                load_a(1).wait()
-
-            own[...] = lax.dot_general(
-                av[n, :, pl.ds(pl.multiple_of(c * HALF, HALF), HALF)],
-                gv[gs],
-                DN,
-                preferred_element_type=jnp.float32,
-            )
-
+            i = t - AT[name]
+
+            @pl.when(jnp.logical_and(i >= 0, i < TILES))
+            def _():
+                steps[name](i)
+
+    def compute(u, part):
+        n, gs = lax.div(u, PER), lax.rem(u, GSLOTS)
+        t = u * PARTS + part
+        if part == 0:
+
+            @pl.when(u + 2 < MATS * PER)
+            def _():
+                load_g(u + 2).start()
+
+            @pl.when(u == 2)
+            def _():
+                load_a(1, 0).start()
+                load_a(1, 1).start()
+
+            load_g(u).wait()
+
+            @pl.when(jnp.logical_or(u == 0, u == PER))
+            def _():
+                load_a(n, 0).wait()
+                load_a(n, 1).wait()
+
+        reuse(copy_d, t)
+
+        def term(half):
+            cols = slice(half * CORE + part * HALF, half * CORE + (part + 1) * HALF)
+            return lax.dot_general(av[n, :, cols], gv[gs], DN, preferred_element_type=jnp.float32)
+
+        d_send[lax.rem(t, SLOTS)] = term(0).astype(jnp.bfloat16)
+        own[lax.rem(u, 2)] = term(1)
+        copy_d(t).start()
+
+    def loop(u, carry):
+        for part in range(PARTS):
+            run(u * PARTS + part)
+            pl.when(u < MATS * PER)(lambda part=part: compute(u, part))
         return carry
 
-    lax.fori_loop(0, TILES + max(AT.values()) // 2, loop, 0)
+    lax.fori_loop(0, (TILES + max(AT.values()) + PARTS - 1) // PARTS, loop, 0)
 
     def finish_staged(i, carry):
         copy_d(i).wait_send()
@@ -319,24 +307,25 @@
 
         return carry
 
-    def finish_shared(i, carry):
-        copy_gc(i).wait_send()
-        copy_ga(i).wait_send()
-        copy_gd(i).wait_send()
-        for k in range(1, ZN):
-
-            @pl.when(jnp.logical_and(has_above, z >= k - 1))
-            def _():
-                copy_gu(k, i, z - k + 1).wait_send()
-
-            @pl.when(jnp.logical_and(has_below, z <= ZN - k))
-            def _():
-                copy_gv(k, i, z + k - 1).wait_send()
-
-        return carry
-
     lax.fori_loop(TILES - SLOTS, TILES, finish_staged, 0)
-    lax.fori_loop(0, TILES, finish_shared, 0)
+
+    def all_of(size, send, recv, dev):
+        ref = out.at[:, 0:size, :]
+        return remote(ref, ref, send, recv, dev)
+
+    all_of(PARTS * PIECE, gcs, gdr, third_peer).wait_send()
+    all_of(PARTS * QUARTER, gas, gdr, first_peer).wait_send()
+    for k in range(1, ZN):
+
+        @pl.when(jnp.logical_and(has_above, z >= k - 1))
+        def _():
+            all_of(PARTS * BLOCK, gus.at[k - 1], gdr, above).wait_send()
+
+        @pl.when(jnp.logical_and(has_below, z <= ZN - k))
+        def _():
+            all_of(PARTS * BLOCK, gvs.at[k - 1], gdr, below).wait_send()
+
+    all_of(PARTS * HALF, gds, gdr, partner).wait()
 
 
 def put(sums, out, sem):
@@ -354,11 +343,11 @@
 
     def step(a, g):
         dma = pltpu.SemaphoreType.DMA
-        one, three = dma((TILES,)), dma((ZN - 1, TILES))
+        one, three = dma((SLOTS,)), dma((ZN - 1, SLOTS))
         scratch = [
             pltpu.VMEM((MATS, TOKENS, D), bf16),
             pltpu.VMEM((GSLOTS, TOKENS, COLS), bf16),
-            pltpu.VMEM((HALF, COLS), f32),
+            pltpu.VMEM((2, HALF, COLS), f32),
             pltpu.VMEM((SLOTS, HALF, COLS), bf16),
             pltpu.VMEM((TILES, HALF, COLS), bf16),
             pltpu.VMEM((SLOTS, QUARTER, COLS), bf16),
@@ -371,11 +360,12 @@
             pltpu.VMEM((SLOTS, PIECE, COLS), bf16),
             pltpu.VMEM((SLOTS, PIECE, COLS), f32),
             pltpu.VMEM((TILES, PIECE, COLS), bf16),
-            dma((3,)),
+            dma((MATS, 2)),
             dma((GSLOTS,)),
         ]
         scratch += [one] * 4 + [three] * 4 + [one] * 2
-        scratch += [one] * 2 + [three] * 4 + [one] * 4
+        hops = dma((ZN - 1,))
+        scratch += [dma, one, hops, three, hops, three, dma, dma((LATE,)), dma, dma]
         sums = pl.pallas_call(
             kernel,
             out_shape=pltpu.VMEM((MATS, D, FF), bf16),

time: 141 us -> 133 us (0.943)
  Pallas kernels: 141 us -> 133 us
    pallas_call x1, Pallas kernels: 136 us -> 128 us  [step(): pl.pallas_call(kernel, out_shape=pltpu.VMEM((MATS, D, FF), bf16), in_spec...]
where the time goes in v2:
time: 133 us
  Pallas kernels  133 us (100%)
    pallas_call x1, Pallas kernels, step(): pl.pallas_call(kernel, out_shape=pltpu.VMEM((MATS, D, FF), bf16), in_spec...  128 us
    pallas_call x1, Pallas kernels, step(): pl.pallas_call(put, out_shape=jax.ShapeDtypeStruct((MATS, D, FF), bf16),...  5 us

profile of v2, /device:TPU:0, one launch (start us, length us, event | category | flops | bytes accessed | tf_op | source)
XLA Modules:
  0.0 132.8 jit_solution(15048021788932735940)
XLA Ops:
  0.0 127.8 %shard_map.28.sums = bf16[2,1024,3328]{2,1,0:T(8,128)(2,1)S(1)} custom-call(bf16[1,2,4096,1024]{3,2,1,0:T(8,128)(2,1)} %a_hbm.1, bf16[1,2,4096,3328]{3,2,1,0:T(8,128)(2,1)} %g_hbm.1), custom_call_target="tpu_custom_call" | custom-call | tf_op jit(solution)/shard_map/pallas_call | solution.py:369
  127.8 5.0 %shard_map.29 = bf16[2,1024,3328]{2,1,0:T(8,128)(2,1)} custom-call(bf16[2,1024,3328]{2,1,0:T(8,128)(2,1)S(1)} %shard_map.28.sums), custom_call_target="tpu_custom_call" | custom-call | tf_op jit(solution)/shard_map/pallas_call | solution.py:379

commit v3 on v2

--- a/solution.py
+++ b/solution.py
@@ -9,24 +9,24 @@
 MATS, TOKENS, D, FF = 2, 4096, 1024, 3328
 COLS = 256
 PER = FF // COLS
-PARTS = 1
-TILES = MATS * PER * PARTS
-CORE = D // 2
-HALF = CORE // PARTS
+TILES = MATS * PER
+HALF = D // 2
+PIECES = 4
+STEP = TOKENS // PIECES
 QUARTER, BLOCK, PIECE = HALF // 2, HALF // 8, HALF // 16
 ZN = 4
 GSLOTS = 3
-SLOTS = 8
-LATE = 32
-ZSLOTS = 12
+SLOTS = 6
+LATE = 12
+ZSLOTS = 9
 PUTS = 8
-AT = dict(a=2, z1=4, z2=5, z3=7, c=9, g0=11, g1=13, g2=15, g3=17, g4=19, g5=29)
+AT = dict(a=3, z1=7, z2=10, z3=13, c=16, g0=19, g1=22, g2=25, g3=29, g4=32, g5=40)
 DN = (((0,), (0,)), ((), ()))
 
 
 def kernel(
     a_hbm, g_hbm, out, av, gv, own, d_send, d_recv, a_send, a_recv, zsum, zu_send, zd_send, zu_recv, zd_recv,
-    c_send, c_keep, c_recv, a_sem, g_sem, ds, dr, xs, xr, us, ur, vs, vr, cs, cr,
+    c_send, c_keep, c_recv, a_sem, g_sem, first_sem, ds, dr, xs, xr, us, ur, vs, vr, cs, cr,
     gcs, gcr, gus, gur, gvs, gvr, gas, gar, gds, gdr,
 ):
     rep, me = lax.axis_index("rep"), lax.axis_index("dp")
@@ -52,16 +52,24 @@
             g_hbm.at[0, n, :, pl.ds(pl.multiple_of(j * COLS, COLS), COLS)], gv.at[s], g_sem.at[s]
         )
 
-    def load_a(n, k):
-        cols = pl.ds(pl.multiple_of((1 - c if k == 0 else c) * CORE, CORE), CORE)
-        return pltpu.make_async_copy(
-            a_hbm.at[0, n, :, cols], av.at[n, :, k * CORE : (k + 1) * CORE], a_sem.at[n, k]
-        )
-
-    load_g(0).start()
-    load_a(0, 0).start()
-    load_a(0, 1).start()
-    load_g(1).start()
+    def load_a(k):
+        cols = pl.ds(pl.multiple_of((1 - c if k == 0 else c) * HALF, HALF), HALF)
+        return pltpu.make_async_copy(a_hbm.at[0, 1, :, cols], av.at[1, :, k * HALF : (k + 1) * HALF], a_sem.at[k])
+
+    def load_first(p):
+        tokens = pl.ds(pl.multiple_of(p * STEP, STEP), STEP)
+        copies = [pltpu.make_async_copy(g_hbm.at[0, 0, tokens, 0:COLS], gv.at[0, tokens, :], first_sem.at[2, p])]
+        for k in range(2):
+            cols = pl.ds(pl.multiple_of((1 - c if k == 0 else c) * HALF, HALF), HALF)
+            copies.append(
+                pltpu.make_async_copy(
+                    a_hbm.at[0, 0, tokens, cols], av.at[0, tokens, k * HALF : (k + 1) * HALF], first_sem.at[k, p]
+                )
+            )
+        return copies
+
+    for copy in load_first(0) + load_first(1):
+        copy.start()
 
     barrier = pltpu.get_barrier_semaphore()
     for dev in (partner, over_x, over_y):
@@ -75,11 +83,40 @@
     def _():
         pl.semaphore_signal(barrier, inc=1, device_id=(rep, below), device_id_type=MESH)
 
-    pl.semaphore_wait(barrier, 3 + has_above.astype(jnp.int32) + has_below.astype(jnp.int32))
 
     def rows(start, size):
         return pl.ds(pl.multiple_of(start, size), size)
 
+    own[...] = jnp.zeros_like(own)
+
+    def piece(k, carry):
+        for copy in load_first(k):
+            copy.wait()
+
+        @pl.when(k + 2 < PIECES)
+        def _():
+            for copy in load_first(k + 2):
+                copy.start()
+
+        @pl.when(k == 1)
+        def _():
+            load_g(1).start()
+
+        tokens = rows(k * STEP, STEP)
+        for slot, mine in ((1, 0), (0, 1)):
+            own[slot] += lax.dot_general(
+                av[0, tokens, mine * HALF : (mine + 1) * HALF],
+                gv[0, tokens, :],
+                DN,
+                preferred_element_type=jnp.float32,
+            )
+        return carry
+
+    lax.fori_loop(0, PIECES, piece, 0)
+    d_send[0] = own[1].astype(jnp.bfloat16)
+
+    pl.semaphore_wait(barrier, 3 + has_above.astype(jnp.int32) + has_below.astype(jnp.int32))
+
     def copy_d(i):
         s = lax.rem(i, SLOTS)
         return remote(d_send.at[s], d_recv.at[i], ds.at[s], dr.at[s], partner)
@@ -101,18 +138,18 @@
         return remote(c_send.at[s], c_recv.at[i], cs.at[s], cr.at[s], third_peer)
 
     def spot(i):
-        n, j = lax.div(i, PER * PARTS), lax.rem(lax.div(i, PARTS), PER)
-        return n, lax.rem(i, PARTS) * HALF, pl.ds(pl.multiple_of(j * COLS, COLS), COLS)
+        n, j = lax.div(i, PER), lax.rem(i, PER)
+        return n, pl.ds(pl.multiple_of(j * COLS, COLS), COLS)
 
     def place(i, start, size):
-        n, row, cols = spot(i)
-        return out.at[n, rows(row + start, size), cols]
+        n, cols = spot(i)
+        return out.at[n, rows(start, size), cols]
 
     def shared(i, start, size, send, recv, dev):
         ref = place(i, start, size)
         return remote(ref, ref, send, recv, dev)
 
-    base_a = c * CORE + first * QUARTER
+    base_a = c * HALF + first * QUARTER
     base_c = base_a + z * BLOCK
 
     def copy_gc(i, mine=True):
@@ -126,11 +163,11 @@
 
     def copy_ga(i, mine=True):
         return shared(
-            i, c * CORE + (first if mine else 1 - first) * QUARTER, QUARTER, gas, gar.at[lax.rem(i, LATE)], first_peer
+            i, c * HALF + (first if mine else 1 - first) * QUARTER, QUARTER, gas, gar.at[lax.rem(i, LATE)], first_peer
         )
 
     def copy_gd(i, mine=True):
-        return shared(i, (c if mine else 1 - c) * CORE, HALF, gds, gdr, partner)
+        return shared(i, (c if mine else 1 - c) * HALF, HALF, gds, gdr, partner)
 
     def reuse(copy, i):
         @pl.when(i >= SLOTS)
@@ -194,8 +231,8 @@
         s = lax.rem(i, SLOTS)
         copy_c(i).wait_recv()
         total = c_keep[s] + c_recv[i].astype(jnp.float32)
-        n, row, cols = spot(i)
-        out[n, rows(row + base_c + third * PIECE, PIECE), cols] = total.astype(jnp.bfloat16)
+        n, cols = spot(i)
+        out[n, rows(base_c + third * PIECE, PIECE), cols] = total.astype(jnp.bfloat16)
         copy_gc(i).start()
 
     def spread(k, i):
@@ -244,52 +281,59 @@
     )
     order = sorted(steps, key=lambda name: -AT[name])
 
-    def run(t):
+    def run(u, half):
         for name in order:
-            i = t - AT[name]
-
-            @pl.when(jnp.logical_and(i >= 0, i < TILES))
-            def _():
-                steps[name](i)
-
-    def compute(u, part):
+            if AT[name] % 2 == half:
+                i = u - AT[name] // 2
+
+                @pl.when(jnp.logical_and(i >= 0, i < TILES))
+                def _():
+                    steps[name](i)
+
+    def term(n, gs, mine, start, size):
+        cols = slice(mine * HALF + start, mine * HALF + start + size)
+        return lax.dot_general(av[n, :, cols], gv[gs], DN, preferred_element_type=jnp.float32)
+
+    def compute(u, half):
         n, gs = lax.div(u, PER), lax.rem(u, GSLOTS)
-        t = u * PARTS + part
-        if part == 0:
-
-            @pl.when(u + 2 < MATS * PER)
+        if half == 0:
+
+            @pl.when(u + 2 < TILES)
             def _():
                 load_g(u + 2).start()
 
             @pl.when(u == 2)
             def _():
-                load_a(1, 0).start()
-                load_a(1, 1).start()
-
-            load_g(u).wait()
-
-            @pl.when(jnp.logical_or(u == 0, u == PER))
-            def _():
-                load_a(n, 0).wait()
-                load_a(n, 1).wait()
-
-        reuse(copy_d, t)
-
-        def term(half):
-            cols = slice(half * CORE + part * HALF, half * CORE + (part + 1) * HALF)
-            return lax.dot_general(av[n, :, cols], gv[gs], DN, preferred_element_type=jnp.float32)
-
-        d_send[lax.rem(t, SLOTS)] = term(0).astype(jnp.bfloat16)
-        own[lax.rem(u, 2)] = term(1)
-        copy_d(t).start()
+                load_a(0).start()
+                load_a(1).start()
+
+            @pl.when(u > 0)
+            def _():
+                load_g(u).wait()
+
+            @pl.when(u == PER)
+            def _():
+                load_a(0).wait()
+                load_a(1).wait()
+
+            reuse(copy_d, u)
+
+        @pl.when(u > 0)
+        def _():
+            start, size = half * HALF // 2, HALF // 2
+            d_send[lax.rem(u, SLOTS), start : start + size] = term(n, gs, 0, start, size).astype(jnp.bfloat16)
+            own[lax.rem(u, 2), start : start + size] = term(n, gs, 1, start, size)
+
+        if half == 1:
+            copy_d(u).start()
 
     def loop(u, carry):
-        for part in range(PARTS):
-            run(u * PARTS + part)
-            pl.when(u < MATS * PER)(lambda part=part: compute(u, part))
+        for half in range(2):
+            run(u, half)
+            pl.when(u < TILES)(lambda half=half: compute(u, half))
         return carry
 
-    lax.fori_loop(0, (TILES + max(AT.values()) + PARTS - 1) // PARTS, loop, 0)
+    lax.fori_loop(0, TILES + max(AT.values()) // 2, loop, 0)
 
     def finish_staged(i, carry):
         copy_d(i).wait_send()
@@ -313,19 +357,19 @@
         ref = out.at[:, 0:size, :]
         return remote(ref, ref, send, recv, dev)
 
-    all_of(PARTS * PIECE, gcs, gdr, third_peer).wait_send()
-    all_of(PARTS * QUARTER, gas, gdr, first_peer).wait_send()
+    all_of(PIECE, gcs, gdr, third_peer).wait_send()
+    all_of(QUARTER, gas, gdr, first_peer).wait_send()
     for k in range(1, ZN):
 
         @pl.when(jnp.logical_and(has_above, z >= k - 1))
         def _():
-            all_of(PARTS * BLOCK, gus.at[k - 1], gdr, above).wait_send()
+            all_of(BLOCK, gus.at[k - 1], gdr, above).wait_send()
 
         @pl.when(jnp.logical_and(has_below, z <= ZN - k))
         def _():
-            all_of(PARTS * BLOCK, gvs.at[k - 1], gdr, below).wait_send()
-
-    all_of(PARTS * HALF, gds, gdr, partner).wait()
+            all_of(BLOCK, gvs.at[k - 1], gdr, below).wait_send()
+
+    all_of(HALF, gds, gdr, partner).wait()
 
 
 def put(sums, out, sem):
@@ -360,8 +404,9 @@
             pltpu.VMEM((SLOTS, PIECE, COLS), bf16),
             pltpu.VMEM((SLOTS, PIECE, COLS), f32),
             pltpu.VMEM((TILES, PIECE, COLS), bf16),
-            dma((MATS, 2)),
+            dma((2,)),
             dma((GSLOTS,)),
+            dma((3, PIECES)),
         ]
         scratch += [one] * 4 + [three] * 4 + [one] * 2
         hops = dma((ZN - 1,))

time: 133 us -> 131 us (0.985)
  Pallas kernels: 133 us -> 131 us
    pallas_call x1, Pallas kernels: 128 us -> 126 us  [step(): pl.pallas_call(kernel, out_shape=pltpu.VMEM((MATS, D, FF), bf16), in_spec...]
where the time goes in v3:
time: 131 us
  Pallas kernels  131 us (100%)
    pallas_call x1, Pallas kernels, step(): pl.pallas_call(kernel, out_shape=pltpu.VMEM((MATS, D, FF), bf16), in_spec...  126 us
    pallas_call x1, Pallas kernels, step(): pl.pallas_call(put, out_shape=jax.ShapeDtypeStruct((MATS, D, FF), bf16),...  5 us

profile of v3, /device:TPU:0, one launch (start us, length us, event | category | flops | bytes accessed | tf_op | source)
XLA Modules:
  0.0 130.5 jit_solution(2907496773800141379)
XLA Ops:
  0.0 125.5 %shard_map.28.sums = bf16[2,1024,3328]{2,1,0:T(8,128)(2,1)S(1)} custom-call(bf16[1,2,4096,1024]{3,2,1,0:T(8,128)(2,1)} %a_hbm.1, bf16[1,2,4096,3328]{3,2,1,0:T(8,128)(2,1)} %g_hbm.1), custom_call_target="tpu_custom_call" | custom-call | tf_op jit(solution)/shard_map/pallas_call | solution.py:414
  125.5 5.0 %shard_map.29 = bf16[2,1024,3328]{2,1,0:T(8,128)(2,1)} custom-call(bf16[2,1024,3328]{2,1,0:T(8,128)(2,1)S(1)} %shard_map.28.sums), custom_call_target="tpu_custom_call" | custom-call | tf_op jit(solution)/shard_map/pallas_call | solution.py:424

commit v4 on v3

--- a/solution.py
+++ b/solution.py
@@ -279,7 +279,7 @@
         g4=step_g4,
         g5=step_g5,
     )
-    order = sorted(steps, key=lambda name: -AT[name])
+    order = sorted(steps, key=lambda name: AT[name])
 
     def run(u, half):
         for name in order:

time: 131 us -> 131 us (level)
  no operation moved by 1% of the time
where the time goes in v4:
time: 131 us; the launch traced here: 130 us
  Pallas kernels  130 us (99%)
    pallas_call x1, Pallas kernels, step(): pl.pallas_call(kernel, out_shape=pltpu.VMEM((MATS, D, FF), bf16), in_spec...  125 us
    pallas_call x1, Pallas kernels, step(): pl.pallas_call(put, out_shape=jax.ShapeDtypeStruct((MATS, D, FF), bf16),...  5 us

profile of v4, /device:TPU:0, one launch (start us, length us, event | category | flops | bytes accessed | tf_op | source)
XLA Modules:
  0.0 130.4 jit_solution(10812623499547241070)
XLA Ops:
  0.0 125.4 %shard_map.28.sums = bf16[2,1024,3328]{2,1,0:T(8,128)(2,1)S(1)} custom-call(bf16[1,2,4096,1024]{3,2,1,0:T(8,128)(2,1)} %a_hbm.1, bf16[1,2,4096,3328]{3,2,1,0:T(8,128)(2,1)} %g_hbm.1), custom_call_target="tpu_custom_call" | custom-call | tf_op jit(solution)/shard_map/pallas_call | solution.py:414
  125.4 5.0 %shard_map.29 = bf16[2,1024,3328]{2,1,0:T(8,128)(2,1)} custom-call(bf16[2,1024,3328]{2,1,0:T(8,128)(2,1)S(1)} %shard_map.28.sums), custom_call_target="tpu_custom_call" | custom-call | tf_op jit(solution)/shard_map/pallas_call | solution.py:424
